TPU v7x, 32 devices: a whole 2x2x4 slice. The times are simulated.
32 devices in a mesh: north: 8 (over z, x), deep: 4 (over y, core).
Axes of the slice: x: 2, y: 2, z: 4, core: 2. Of those that a mesh axis runs over, the one named last changes fastest.
Arguments:
- source: float32 [128, 128, 2048], P(None, 'north', 'deep'), may hold values from -6 to 6
- symbol_x: float32 [128], replicated, may hold values from 0.3 to 3
- symbol_y: float32 [128], replicated, may hold values from 0.3 to 3
- symbol_z: float32 [2048], replicated, may hold values from 0.3 to 3
Outputs:
- coefficients: float32 [64, 64, 1024], P('north', 'deep')
All inputs are finite; a program needn't handle non-finite values.
Results may differ from a plain program's by a relative error of at most 0.000071.
Values sent between devices are 32-bit elements; how exact they have to be, the bound alone decides.
A program may use at most 128 MiB of HBM per device.

v0:
```python
import jax
import jax.numpy as jnp
import numpy as np
from jax import lax
from jax.sharding import PartitionSpec as P

HIGH = lax.Precision.HIGH


def small_table(rows, modes, count):
    rank = np.outer(rows, modes) % (2 * count + 2)
    return np.pi / (count + 1) * rank


def kept_table(count):
    angle = small_table(np.arange(1, count + 1), np.arange(1, count // 2 + 1), count)
    return jnp.asarray((np.sin(angle) * (2.0 / (count + 1)) ** 0.5).astype(np.float32))


def long_table(count, fine=32):
    modes = np.arange(1, count // 2 + 1)
    gain = (2.0 / (count + 1)) ** 0.5
    coarse = small_table(np.arange(0, count, fine), modes, count)
    step = small_table(np.arange(1, fine + 1), modes, count)
    f32 = lambda v: jnp.asarray(v.astype(np.float32))
    sin_a, cos_a = (f32(np.sin(coarse) * gain), f32(np.cos(coarse) * gain))
    sin_b, cos_b = (f32(np.sin(step)), f32(np.cos(step)))
    table = sin_a[:, None, :] * cos_b[None] + cos_a[:, None, :] * sin_b[None]
    return table.reshape(count, count // 2)


def on_device(source, symbol_x, symbol_y, symbol_z):
    north, deep = (lax.axis_size("north"), lax.axis_size("deep"))
    nx, ny_part, nz_part = source.shape
    each = nx // 2 // north // deep
    v = jnp.einsum("xk,xyz->kyz", kept_table(nx), source, precision=HIGH)
    v = v.reshape(north, deep, each, ny_part, nz_part)
    v = lax.all_to_all(v, "deep", split_axis=1, concat_axis=4, tiled=True)
    v = v.reshape(north, each, ny_part, nz_part * deep)
    v = jnp.einsum("neyz,zk->neyk", v, long_table(nz_part * deep), precision=HIGH)
    v = lax.all_to_all(v, "north", split_axis=0, concat_axis=2, tiled=True)
    v = v.reshape(each, ny_part * north, v.shape[-1])
    v = jnp.einsum("eyz,yk->ekz", v, kept_table(ny_part * north), precision=HIGH)
    v = lax.all_to_all(v, "deep", split_axis=1, concat_axis=0, tiled=True)
    part_x = lax.dynamic_slice_in_dim(symbol_x, lax.axis_index("north") * v.shape[0], v.shape[0])
    part_y = lax.dynamic_slice_in_dim(symbol_y, lax.axis_index("deep") * v.shape[1], v.shape[1])
    symbol = part_x[:, None, None] + part_y[None, :, None] + symbol_z[: v.shape[2]][None, None, :]
    return v * lax.rsqrt(symbol)


def solution(mesh):
    in_specs = (P(None, "north", "deep"), P(), P(), P())
    out_specs = P("north", "deep", None)
    return jax.shard_map(
        on_device, mesh=mesh, in_specs=in_specs, out_specs=out_specs, check_vma=False
    )
```

profile of v0, /device:TPU:0, one launch (start us, length us, event | category | flops | bytes accessed | tf_op | source)
XLA Modules:
  0.0 101.3 jit_solution(16082460734918682209)
XLA Ops:
  0.0 5.6 %fusion = f32[64,16,512]{2,0,1:T(8,128)S(1)} fusion(f32[128,64,1]{0,1,2:T(8,128)} %constant.32, f32[128,16,512]{2,1,0:T(8,128)} %param.10), kind=kOutput, calls=%fused_computation.1 | convolution fusion | flops 402653184 | bytes 6324224 | tf_op jit(solution)/shard_map/xk,xyz->kyz/dot_general | solution.py:36
  5.7 2.3 %reshape.69 = f32[8,4,2,16,512]{4,2,1,0,3:T(2,128)} reshape(f32[64,16,512]{2,0,1:T(8,128)S(1)} %fusion) | data formatting | bytes 4194304 | tf_op jit(solution)/shard_map/reshape | solution.py:37
  7.9 4.3 %copy.19 = f32[8,4,2,16,512]{4,2,0,3,1:T(2,128)} copy(f32[8,4,2,16,512]{4,2,1,0,3:T(2,128)} %reshape.69) | data formatting | bytes 4194304 | tf_op jit(solution)/shard_map/reshape | solution.py:37
  12.2 4.3 %all-to-all-start = ((f32[8,4,2,16,512]{4,2,0,3,1:T(2,128)}), f32[8,4,2,16,512]{4,2,0,3,1:T(2,128)S(1)}, u32[]{:S(2)}, u32[]{:S(2)}) async-start(f32[8,4,2,16,512]{4,2,0,3,1:T(2,128)} %copy.19), calls=%async_computation | async-start | bytes 4194304 | tf_op jit(solution)/shard_map/all_to_all | solution.py:38
  16.5 4.6 %multiply_add_fusion = f32[64,32,1024]{2,1,0:T(8,128)} fusion(f32[32,1024]{1,0:T(8,128)S(1)} %copy-done.2, f32[64,1024]{1,0:T(8,128)S(1)} %copy-done, f32[32,1024]{1,0:T(8,128)S(1)} %copy-done.3, f32[64,1024]{1,0:T(8,128)S(1)} %copy-done.1), kind=kLoop, calls=%fused_computation | loop fusion | flops 6291456 | bytes 9175040 | tf_op jit(solution)/shard_map/add | solution.py:28
  21.1 21.0 %all-to-all-done = f32[8,4,2,16,512]{4,2,0,3,1:T(2,128)S(1)} async-done(((f32[8,4,2,16,512]{4,2,0,3,1:T(2,128)}), f32[8,4,2,16,512]{4,2,0,3,1:T(2,128)S(1)}, u32[]{:S(2)}, u32[]{:S(2)}) %all-to-all-start) | async-done | bytes 2097184 | tf_op jit(solution)/shard_map/all_to_all | solution.py:38
  42.2 2.7 %copy.20 = f32[8,1,2,16,4,512]{5,4,3,2,0,1:T(4,128)} copy(f32[8,1,2,16,4,512]{5,2,0,3,4,1:T(2,128)S(1)} %bitcast.30) | data formatting | bytes 4194304 | tf_op jit(solution)/shard_map/all_to_all | solution.py:38
  44.9 2.7 %reshape.70 = f32[8,2,16,2048]{3,2,1,0:T(8,128)S(1)} reshape(f32[8,1,2,16,4,512]{5,4,3,2,0,1:T(4,128)} %copy.20) | data formatting | bytes 4194304 | tf_op jit(solution)/shard_map/reshape | solution.py:39
  47.6 6.5 %fusion.2 = f32[8,2,16,1024]{3,2,1,0:T(8,128)S(1)} fusion(f32[8,2,16,2048]{3,2,1,0:T(8,128)S(1)} %reshape.70, f32[2048,1024,1,1]{1,0,3,2:T(8,128)} %bitcast.29), kind=kOutput, calls=%fused_computation.6 | convolution fusion | flops 3221225472 | bytes 11534336 | tf_op jit(solution)/shard_map/neyz,zk->neyk/dot_general | solution.py:40
  54.0 0.0 copy-start.4
  54.1 0.0 copy-start.5
  54.1 0.0 copy-start.6
  54.1 0.0 slice-start
  54.1 32.0 %all_to_all.48 = f32[8,2,16,1024]{3,2,1,0:T(8,128)S(1)} all-to-all(f32[8,2,16,1024]{3,2,1,0:T(8,128)S(1)} %fusion.2), channel_id=1, replica_groups=mesh['north'=8,'deep'=4] {'north'}, dimensions={0} | all-to-all | bytes 2097152 | tf_op jit(solution)/shard_map/all_to_all | solution.py:41
  86.1 0.1 copy.21
  86.2 0.4 convolution_bitcast_fusion
  86.7 1.2 %copy.22 = f32[2,64,1024]{2,0,1:T(2,128)} copy(f32[2,64,1024]{2,1,0:T(8,128)S(1)} %convolution_bitcast_fusion) | data formatting | bytes 1048576 | tf_op jit(solution)/shard_map/eyz,yk->ekz/transpose | solution.py:43
  87.9 3.5 %all-to-all-start.2 = ((f32[2,64,1024]{2,0,1:T(2,128)}), f32[2,64,1024]{2,0,1:T(2,128)S(1)}, u32[]{:S(2)}, u32[]{:S(2)}) async-start(f32[2,64,1024]{2,0,1:T(2,128)} %copy.22), calls=%async_computation.2 | async-start | bytes 1048576 | tf_op jit(solution)/shard_map/all_to_all | solution.py:44
  91.4 0.1 dynamic_slice.7
  91.5 0.1 dynamic_slice.6
  91.5 0.1 broadcast_add_fusion
  91.6 8.5 %all-to-all-done.2 = f32[2,64,1024]{2,0,1:T(2,128)S(1)} async-done(((f32[2,64,1024]{2,0,1:T(2,128)}), f32[2,64,1024]{2,0,1:T(2,128)S(1)}, u32[]{:S(2)}, u32[]{:S(2)}) %all-to-all-start.2) | async-done | bytes 524320 | tf_op jit(solution)/shard_map/all_to_all | solution.py:44
  100.1 0.2 copy.23
  100.3 0.9 bitcast_multiply_fusion
  (12 shorter events, 0.0 us)
Async XLA Ops:
  7.9 8.5 %copy-start = (f32[64,1024]{1,0:T(8,128)S(1)}, f32[64,1024]{1,0:T(8,128)}, u32[]{:S(2)}) copy-start(f32[64,1024]{1,0:T(8,128)} %constant.29.clone) | copy-start | bytes 786436
  7.9 8.5 %copy-start.1 = (f32[64,1024]{1,0:T(8,128)S(1)}, f32[64,1024]{1,0:T(8,128)}, u32[]{:S(2)}) copy-start(f32[64,1024]{1,0:T(8,128)} %constant.28.clone) | copy-start | bytes 786436
  7.9 8.5 %copy-start.2 = (f32[32,1024]{1,0:T(8,128)S(1)}, f32[32,1024]{1,0:T(8,128)}, u32[]{:S(2)}) copy-start(f32[32,1024]{1,0:T(8,128)} %constant.30.clone) | copy-start | bytes 393220
  7.9 8.6 %copy-start.3 = (f32[32,1024]{1,0:T(8,128)S(1)}, f32[32,1024]{1,0:T(8,128)}, u32[]{:S(2)}) copy-start(f32[32,1024]{1,0:T(8,128)} %constant.31.clone) | copy-start | bytes 393220
  12.2 29.9 %all-to-all-start = ((f32[8,4,2,16,512]{4,2,0,3,1:T(2,128)}), f32[8,4,2,16,512]{4,2,0,3,1:T(2,128)S(1)}, u32[]{:S(2)}, u32[]{:S(2)}) async-start(f32[8,4,2,16,512]{4,2,0,3,1:T(2,128)} %copy.19), calls=%async_computation | async-start | bytes 4194304 | tf_op jit(solution)/shard_map/all_to_all | solution.py:38
  54.0 32.2 %copy-start.4 = (f32[128,64,1]{0,1,2:T(8,128)S(1)}, f32[128,64,1]{0,1,2:T(8,128)}, u32[]{:S(2)}) copy-start(f32[128,64,1]{0,1,2:T(8,128)} %constant.32) | copy-start | bytes 98308
  54.1 37.3 %copy-start.5 = (f32[128]{0:T(128)S(1)}, f32[128]{0:T(128)}, u32[]{:S(2)}) copy-start(f32[128]{0:T(128)} %param.12) | copy-start | bytes 1540
  54.1 37.4 %copy-start.6 = (f32[128]{0:T(128)S(1)}, f32[128]{0:T(128)}, u32[]{:S(2)}) copy-start(f32[128]{0:T(128)} %param.11) | copy-start | bytes 1540
  54.1 46.2 %slice-start = ((f32[2048]{0:T(1024)}), f32[1024]{0:T(1024)S(1)}, s32[]{:S(2)}) async-start(f32[2048]{0:T(1024)} %param.13), calls=%async_computation.3 | async-start | bytes 8192 | tf_op jit(solution)/shard_map/slice | solution.py:47
  87.9 12.3 %all-to-all-start.2 = ((f32[2,64,1024]{2,0,1:T(2,128)}), f32[2,64,1024]{2,0,1:T(2,128)S(1)}, u32[]{:S(2)}, u32[]{:S(2)}) async-start(f32[2,64,1024]{2,0,1:T(2,128)} %copy.22), calls=%async_computation.2 | async-start | bytes 1048576 | tf_op jit(solution)/shard_map/all_to_all | solution.py:44
where the time goes:
time: 102 us; the launch traced here: 101 us
  blocking collectives  32 us (31%)
  waiting for transfers between devices  29.6 us (29%)
  local copies, waits for them, and re-layouts  13.6 us (13%)
  matrix products  12.5 us (12%)
  starting transfers between devices  7.74 us (8%)
  other arithmetic  5.65 us (6%)
    all_to_all x1, blocking collectives, on_device(): v = lax.all_to_all(v, 'north', split_axis=0, concat_axis=2, tiled=True)  32 us
    all_to_all x1, waiting for transfers between devices, on_device(): v = lax.all_to_all(v, 'deep', split_axis=1, concat_axis=4, tiled=True)  21 us
    all_to_all x1, waiting for transfers between devices, on_device(): v = lax.all_to_all(v, 'deep', split_axis=1, concat_axis=0, tiled=True)  8.54 us
    reshape x2, local copies, waits for them, and re-layouts, on_device(): v = v.reshape(north, deep, each, ny_part, nz_part)  6.54 us
    dot_general x1, matrix products, on_device(): jnp.einsum('neyz,zk->neyk', v, long_table(nz_part * deep), precision=HIGH)  6.47 us
    dot_general x1, matrix products, on_device(): v = jnp.einsum('xk,xyz->kyz', kept_table(nx), source, precision=HIGH)  5.65 us
    add x1, other arithmetic, long_table(): table = sin_a[:, None, :] * cos_b[None] + cos_a[:, None, :] * sin_b[None]  4.63 us
    all_to_all x1, starting transfers between devices, on_device(): v = lax.all_to_all(v, 'deep', split_axis=1, concat_axis=4, tiled=True)  4.27 us
  transfers between devices with their start and end apart: 2, of which 2 were waited for; matrix products, arithmetic and copies ran while one was open for 5% of the time, Pallas kernels for 0%

commit v1 on v0

--- a/solution.py
+++ b/solution.py
@@ -38,7 +38,10 @@
     v = lax.all_to_all(v, "deep", split_axis=1, concat_axis=4, tiled=True)
     v = v.reshape(north, each, ny_part, nz_part * deep)
     v = jnp.einsum("neyz,zk->neyk", v, long_table(nz_part * deep), precision=HIGH)
-    v = lax.all_to_all(v, "north", split_axis=0, concat_axis=2, tiled=True)
+    v = jnp.concatenate(
+        lax.all_to_all(jnp.stack(jnp.split(v, lax.axis_size("north"), axis=0)), "north", 0, 0),
+        axis=2,
+    )
     v = v.reshape(each, ny_part * north, v.shape[-1])
     v = jnp.einsum("eyz,yk->ekz", v, kept_table(ny_part * north), precision=HIGH)
     v = lax.all_to_all(v, "deep", split_axis=1, concat_axis=0, tiled=True)

time: 102 us -> 102 us (level)
  no operation moved by 1% of the time
where the time goes in v1:
time: 102 us; the launch traced here: 101 us
  blocking collectives  31.9 us (31%)
  waiting for transfers between devices  29.6 us (29%)
  local copies, waits for them, and re-layouts  13.7 us (13%)
  matrix products  12.5 us (12%)
  starting transfers between devices  7.74 us (8%)
  other arithmetic  5.65 us (6%)
    all_to_all x1, blocking collectives, on_device(): lax.all_to_all(jnp.stack(jnp.split(v, lax.axis_size('north'), axis=0)), '...  31.9 us
    all_to_all x1, waiting for transfers between devices, on_device(): v = lax.all_to_all(v, 'deep', split_axis=1, concat_axis=4, tiled=True)  21 us
    all_to_all x1, waiting for transfers between devices, on_device(): v = lax.all_to_all(v, 'deep', split_axis=1, concat_axis=0, tiled=True)  8.54 us
    reshape x2, local copies, waits for them, and re-layouts, on_device(): v = v.reshape(north, deep, each, ny_part, nz_part)  6.54 us
    dot_general x1, matrix products, on_device(): jnp.einsum('neyz,zk->neyk', v, long_table(nz_part * deep), precision=HIGH)  6.47 us
    dot_general x1, matrix products, on_device(): v = jnp.einsum('xk,xyz->kyz', kept_table(nx), source, precision=HIGH)  5.65 us
    add x1, other arithmetic, long_table(): table = sin_a[:, None, :] * cos_b[None] + cos_a[:, None, :] * sin_b[None]  4.63 us
    all_to_all x1, starting transfers between devices, on_device(): v = lax.all_to_all(v, 'deep', split_axis=1, concat_axis=4, tiled=True)  4.27 us
  transfers between devices with their start and end apart: 2, of which 2 were waited for; matrix products, arithmetic and copies ran while one was open for 5% of the time, Pallas kernels for 0%

profile of v1, /device:TPU:0, one launch (start us, length us, event | category | flops | bytes accessed | tf_op | source)
XLA Modules:
  0.0 101.3 jit_solution(593309127478340535)
XLA Ops:
  0.0 5.6 %fusion = f32[64,16,512]{2,0,1:T(8,128)S(1)} fusion(f32[128,64,1]{0,1,2:T(8,128)} %constant.32, f32[128,16,512]{2,1,0:T(8,128)} %param.10), kind=kOutput, calls=%fused_computation.1 | convolution fusion | flops 402653184 | bytes 6324224 | tf_op jit(solution)/shard_map/xk,xyz->kyz/dot_general | solution.py:36
  5.7 2.3 %reshape.68 = f32[8,4,2,16,512]{4,2,1,0,3:T(2,128)} reshape(f32[64,16,512]{2,0,1:T(8,128)S(1)} %fusion) | data formatting | bytes 4194304 | tf_op jit(solution)/shard_map/reshape | solution.py:37
  7.9 4.3 %copy.19 = f32[8,4,2,16,512]{4,2,0,3,1:T(2,128)} copy(f32[8,4,2,16,512]{4,2,1,0,3:T(2,128)} %reshape.68) | data formatting | bytes 4194304 | tf_op jit(solution)/shard_map/reshape | solution.py:37
  12.2 4.3 %all-to-all-start = ((f32[8,4,2,16,512]{4,2,0,3,1:T(2,128)}), f32[8,4,2,16,512]{4,2,0,3,1:T(2,128)S(1)}, u32[]{:S(2)}, u32[]{:S(2)}) async-start(f32[8,4,2,16,512]{4,2,0,3,1:T(2,128)} %copy.19), calls=%async_computation | async-start | bytes 4194304 | tf_op jit(solution)/shard_map/all_to_all | solution.py:38
  16.5 4.6 %multiply_add_fusion = f32[64,32,1024]{2,1,0:T(8,128)} fusion(f32[32,1024]{1,0:T(8,128)S(1)} %copy-done.2, f32[64,1024]{1,0:T(8,128)S(1)} %copy-done.1, f32[32,1024]{1,0:T(8,128)S(1)} %copy-done.3, f32[64,1024]{1,0:T(8,128)S(1)} %copy-done), kind=kLoop, calls=%fused_computation | loop fusion | flops 6291456 | bytes 9175040 | tf_op jit(solution)/shard_map/add | solution.py:28
  21.1 21.0 %all-to-all-done = f32[8,4,2,16,512]{4,2,0,3,1:T(2,128)S(1)} async-done(((f32[8,4,2,16,512]{4,2,0,3,1:T(2,128)}), f32[8,4,2,16,512]{4,2,0,3,1:T(2,128)S(1)}, u32[]{:S(2)}, u32[]{:S(2)}) %all-to-all-start) | async-done | bytes 2097184 | tf_op jit(solution)/shard_map/all_to_all | solution.py:38
  42.2 2.7 %copy.20 = f32[8,1,2,16,4,512]{5,4,3,2,0,1:T(4,128)} copy(f32[8,1,2,16,4,512]{5,2,0,3,4,1:T(2,128)S(1)} %bitcast.60) | data formatting | bytes 4194304 | tf_op jit(solution)/shard_map/all_to_all | solution.py:38
  44.9 2.7 %reshape.69 = f32[8,2,16,2048]{3,2,1,0:T(8,128)S(1)} reshape(f32[8,1,2,16,4,512]{5,4,3,2,0,1:T(4,128)} %copy.20) | data formatting | bytes 4194304 | tf_op jit(solution)/shard_map/reshape | solution.py:39
  47.6 6.5 %fusion.10 = f32[8,2,16,1024]{3,2,1,0:T(8,128)S(1)} fusion(f32[8,2,16,2048]{3,2,1,0:T(8,128)S(1)} %reshape.69, f32[2048,1024,1,1]{1,0,3,2:T(8,128)} %bitcast.59), kind=kOutput, calls=%fused_computation.22 | convolution fusion | flops 3221225472 | bytes 11534336 | tf_op jit(solution)/shard_map/neyz,zk->neyk/dot_general | solution.py:40
  54.0 0.0 copy-start.4
  54.2 0.0 copy-start.5
  54.2 0.0 copy-start.6
  54.2 0.0 slice-start
  54.3 31.9 %all_to_all.38 = f32[8,1,2,16,1024]{4,3,2,1,0:T(8,128)S(1)} all-to-all(f32[8,1,2,16,1024]{4,3,2,1,0:T(8,128)S(1)} %fusion.2), channel_id=1, replica_groups=mesh['north'=8,'deep'=4] {'north'}, dimensions={0} | all-to-all | bytes 2097152 | tf_op jit(solution)/shard_map/all_to_all | solution.py:42
  86.2 0.1 copy.21
  86.3 0.4 convolution_bitcast_fusion
  86.7 1.2 %copy.22 = f32[2,64,1024]{2,0,1:T(2,128)} copy(f32[2,64,1024]{2,1,0:T(8,128)S(1)} %convolution_bitcast_fusion) | data formatting | bytes 1048576 | tf_op jit(solution)/shard_map/eyz,yk->ekz/transpose | solution.py:46
  87.9 3.5 %all-to-all-start.2 = ((f32[2,64,1024]{2,0,1:T(2,128)}), f32[2,64,1024]{2,0,1:T(2,128)S(1)}, u32[]{:S(2)}, u32[]{:S(2)}) async-start(f32[2,64,1024]{2,0,1:T(2,128)} %copy.22), calls=%async_computation.2 | async-start | bytes 1048576 | tf_op jit(solution)/shard_map/all_to_all | solution.py:47
  91.4 0.1 dynamic_slice.6
  91.5 0.1 dynamic_slice.7
  91.5 0.1 broadcast_add_fusion
  91.6 8.5 %all-to-all-done.2 = f32[2,64,1024]{2,0,1:T(2,128)S(1)} async-done(((f32[2,64,1024]{2,0,1:T(2,128)}), f32[2,64,1024]{2,0,1:T(2,128)S(1)}, u32[]{:S(2)}, u32[]{:S(2)}) %all-to-all-start.2) | async-done | bytes 524320 | tf_op jit(solution)/shard_map/all_to_all | solution.py:47
  100.2 0.2 copy.23
  100.3 0.9 bitcast_multiply_fusion
  (20 shorter events, 0.1 us)
Async XLA Ops:
  7.9 8.5 %copy-start = (f32[64,1024]{1,0:T(8,128)S(1)}, f32[64,1024]{1,0:T(8,128)}, u32[]{:S(2)}) copy-start(f32[64,1024]{1,0:T(8,128)} %constant.28.clone) | copy-start | bytes 786436
  7.9 8.5 %copy-start.1 = (f32[64,1024]{1,0:T(8,128)S(1)}, f32[64,1024]{1,0:T(8,128)}, u32[]{:S(2)}) copy-start(f32[64,1024]{1,0:T(8,128)} %constant.29.clone) | copy-start | bytes 786436
  7.9 8.5 %copy-start.2 = (f32[32,1024]{1,0:T(8,128)S(1)}, f32[32,1024]{1,0:T(8,128)}, u32[]{:S(2)}) copy-start(f32[32,1024]{1,0:T(8,128)} %constant.30.clone) | copy-start | bytes 393220
  7.9 8.6 %copy-start.3 = (f32[32,1024]{1,0:T(8,128)S(1)}, f32[32,1024]{1,0:T(8,128)}, u32[]{:S(2)}) copy-start(f32[32,1024]{1,0:T(8,128)} %constant.31.clone) | copy-start | bytes 393220
  12.2 29.9 %all-to-all-start = ((f32[8,4,2,16,512]{4,2,0,3,1:T(2,128)}), f32[8,4,2,16,512]{4,2,0,3,1:T(2,128)S(1)}, u32[]{:S(2)}, u32[]{:S(2)}) async-start(f32[8,4,2,16,512]{4,2,0,3,1:T(2,128)} %copy.19), calls=%async_computation | async-start | bytes 4194304 | tf_op jit(solution)/shard_map/all_to_all | solution.py:38
  54.0 32.2 %copy-start.4 = (f32[128,64,1]{0,1,2:T(8,128)S(1)}, f32[128,64,1]{0,1,2:T(8,128)}, u32[]{:S(2)}) copy-start(f32[128,64,1]{0,1,2:T(8,128)} %constant.32) | copy-start | bytes 98308
  54.2 37.2 %copy-start.5 = (f32[128]{0:T(128)S(1)}, f32[128]{0:T(128)}, u32[]{:S(2)}) copy-start(f32[128]{0:T(128)} %param.11) | copy-start | bytes 1540
  54.2 37.3 %copy-start.6 = (f32[128]{0:T(128)S(1)}, f32[128]{0:T(128)}, u32[]{:S(2)}) copy-start(f32[128]{0:T(128)} %param.12) | copy-start | bytes 1540
  54.2 46.1 %slice-start = ((f32[2048]{0:T(1024)}), f32[1024]{0:T(1024)S(1)}, s32[]{:S(2)}) async-start(f32[2048]{0:T(1024)} %param.13), calls=%async_computation.3 | async-start | bytes 8192 | tf_op jit(solution)/shard_map/slice | solution.py:50
  87.9 12.3 %all-to-all-start.2 = ((f32[2,64,1024]{2,0,1:T(2,128)}), f32[2,64,1024]{2,0,1:T(2,128)S(1)}, u32[]{:S(2)}, u32[]{:S(2)}) async-start(f32[2,64,1024]{2,0,1:T(2,128)} %copy.22), calls=%async_computation.2 | async-start | bytes 1048576 | tf_op jit(solution)/shard_map/all_to_all | solution.py:47
